TPU v7x, 256 devices: a whole 4x4x8 slice. The times are simulated.
256 devices in a mesh: gx: 32 (over z, y_lo, core), gy: 8 (over y_hi, x).
Axes of the slice: x: 4, y: 4 (y_hi: 2, y_lo: 2; y = y_hi * 2 + y_lo), z: 8, core: 2. Of those that a mesh axis runs over, the one named last changes fastest.
Arguments:
- right_side: float32 [32, 8, 512, 256], P('gx', 'gy'), may hold values from -8 to 8, as said below
- coords: float32 [32, 8, 2, 512], P('gx', 'gy'), may hold values from 0 to 1
- noise: float32 [32, 8, 512], P('gx', 'gy'), may hold values from 0.25 to 1
- intersect: int32 [32, 8, 128], P('gx', 'gy'), may hold values from 0 to 4607, as said below
Outputs:
- solution: float32 [32, 8, 512, 256], P('gx', 'gy')
- residual: float32 [32, 8, 512, 256], P('gx', 'gy')
Inputs may be any that keep to these rules, and one draw needn't show every extreme that they name: `right_side`: right-hand sides of order one. `intersect`: each subdomain's list holds 128 distinct indices in increasing order; none names the subdomain itself (block number 4) or a subdomain beyond the first or last one along the second dimension.
All inputs are finite; a program needn't handle non-finite values.
Results may differ from a plain program's by a relative error of at most 0.0003.
Values sent between devices are 32-bit elements; how exact they have to be, the bound alone decides.
A program may use at most 128 MiB of HBM per device.

v0:
```python
import math
import jax
import jax.numpy as jnp
from jax import lax
from jax.sharding import Mesh
from jax.sharding import PartitionSpec as P

ITERS = 3
GX = ("gx_0", "gx_1", "gx_2")
GY = ("gy_0", "gy_1")
GX_GY = ("gx_0", "gx_1", "gx_2", "gy_0", "gy_1")
RANGE_LEN = 0.25
ROOT_THREE = math.sqrt(3.0)
HIGH = lax.Precision.HIGHEST


def shifted(value, axis, by):
    count = lax.axis_size(axis)
    return lax.ppermute(value, axis, [(i, (i + by) % count) for i in range(count)])


def passed_along(block, axis, distance):
    devices = range(lax.axis_size(axis))
    route = [(i - distance, i) for i in devices if i - distance in devices]
    return lax.ppermute(block, axis, route)


def over_axes(value, axes):
    for axis in axes:
        value = lax.psum(value, axis)
    return value


def kernel_block(rows_pos, cols_pos):
    delta_x = rows_pos[0][:, None] - cols_pos[0][None, :]
    delta_y = rows_pos[1][:, None] - cols_pos[1][None, :]
    distance = jnp.sqrt(delta_x * delta_x + delta_y * delta_y)
    scaled = ROOT_THREE / RANGE_LEN * distance
    clipped = jnp.minimum(distance, 1.0)
    taper_val = jnp.square(jnp.square(1.0 - clipped)) * (4.0 * clipped + 1.0)
    return (1.0 + scaled) * jnp.exp(-scaled) * taper_val


def window_values(values):
    beside = {}
    for step_by in (1, -1):
        beside[step_by] = shifted(values, GX, step_by)
    column = jnp.stack([beside[1], values, beside[-1]])
    across = {}
    for step_by in (1, -1):
        across[step_by] = passed_along(column, GY, step_by)
    return [across[1], column, across[-1]]


def window_index(values):
    beside = {}
    for step_by in (1, -1):
        beside[step_by] = shifted(values, GX, step_by)
    column = jnp.stack([beside[1], values, beside[-1]])
    across = {}
    for step_by in (1, -1):
        across[step_by] = passed_along(column, GY, step_by)
    return [across[1], column, across[-1]]


def column_sum(first, second):
    return jnp.sum(first * second, axis=0)


def both_sums(residue, precond, image_vec):
    return (
        over_axes(column_sum(residue, precond), GX_GY),
        over_axes(column_sum(image_vec, precond), GX_GY),
    )


def shards(right_side, coords, noise, intersect):
    points = right_side.shape[2]
    rhs_count = right_side.shape[3]
    intersect_len = intersect.shape[2]
    ext_len = points + intersect_len
    own_pos = coords.reshape(2, points)
    own_noise = noise.reshape(points)
    point_info = jnp.concatenate([own_pos, own_noise[None, :]], axis=0)
    info_cols = window_values(point_info)
    positions = [
        [
            jnp.stack(
                [
                    info_cols[col_off][row_off, 0] + float(row_off - 1),
                    info_cols[col_off][row_off, 1] + float(col_off - 1),
                ]
            )
            for col_off in range(3)
        ]
        for row_off in range(3)
    ]
    intersect_ids = intersect.reshape(intersect_len)
    block_id = intersect_ids // points
    row_in = intersect_ids % points
    row_of = block_id // 3
    col_of = block_id % 3
    local_id = row_of * points + row_in
    picked_info = [
        jnp.take(
            jnp.transpose(info_cols[col_off], (1, 0, 2)).reshape(3, 3 * points), local_id, axis=1
        )
        for col_off in range(3)
    ]
    chosen = jnp.where(
        col_of[None, :] == 0,
        picked_info[0],
        jnp.where(col_of[None, :] == 1, picked_info[1], picked_info[2]),
    )
    ov_pos = jnp.stack(
        [chosen[0] + (row_of - 1).astype(jnp.float32), chosen[1] + (col_of - 1).astype(jnp.float32)]
    )
    ext_pos = jnp.concatenate([own_pos, ov_pos], axis=1)
    ext_noise = jnp.concatenate([own_noise, chosen[2]])
    local_matrix = kernel_block(ext_pos, ext_pos) + jnp.diag(ext_noise)
    factor = jnp.linalg.cholesky(local_matrix)
    inv_factor = lax.linalg.triangular_solve(
        factor, jnp.eye(ext_len, dtype=jnp.float32), left_side=True, lower=True
    )
    inverse = jnp.dot(inv_factor.T, inv_factor, precision=HIGH, preferred_element_type=jnp.float32)
    near_ids = window_index(intersect_ids)
    point_iota = jnp.arange(points, dtype=jnp.int32)[:, None]
    row_base = (2 - jnp.arange(3, dtype=jnp.int32))[:, None] * 3
    selectors = []
    for col_off in range(3):
        own_rows = near_ids[col_off] - (row_base + (2 - col_off)) * points
        selectors.append((point_iota == own_rows.reshape(1, 3 * intersect_len)).astype(jnp.float32))

    def borrowed_rows(residue):
        requested = [
            lax.dot_general(
                selectors[col_off],
                residue,
                (((0,), (0,)), ((), ())),
                precision=HIGH,
                preferred_element_type=jnp.float32,
            ).reshape(3, intersect_len, rhs_count)
            for col_off in range(3)
        ]
        combined = jnp.stack([requested[col_off][1] for col_off in range(3)])
        for step_by, row_off in ((-1, 0), (1, 2)):
            outgoing = jnp.stack([requested[col_off][row_off] for col_off in range(3)])
            combined = combined + shifted(outgoing, GX, step_by)
        gathered = combined[1]
        for step_by, col_off in ((-1, 0), (1, 2)):
            gathered = gathered + passed_along(combined[col_off], GY, step_by)
        return gathered

    def precondition(residue):
        gathered = borrowed_rows(residue)
        extended = jnp.concatenate([residue, gathered], axis=0)
        solved = jnp.dot(inverse, extended, precision=HIGH, preferred_element_type=jnp.float32)
        returned = window_values(solved[points:])
        result = solved[:points]
        for col_off in range(3):
            result = result + jnp.dot(
                selectors[col_off],
                returned[col_off].reshape(3 * intersect_len, rhs_count),
                precision=HIGH,
                preferred_element_type=jnp.float32,
            )
        return result

    noise_col = own_noise[:, None]

    def operate(vector):
        columns = window_values(vector)
        accumulated = noise_col * vector
        for row_off in range(3):
            for col_off in range(3):
                accumulated = accumulated + jnp.dot(
                    kernel_block(own_pos, positions[row_off][col_off]),
                    columns[col_off][row_off],
                    precision=HIGH,
                    preferred_element_type=jnp.float32,
                )
        return accumulated

    residual = right_side.reshape(points, rhs_count)
    solution = jnp.zeros_like(residual)
    precond = precondition(residual)
    image_vec = operate(precond)
    gamma_now, curv_sum = both_sums(residual, precond, image_vec)
    step_size = gamma_now / curv_sum
    direction = precond
    image_dir = image_vec
    for iteration in range(ITERS):
        solution = solution + step_size * direction
        residual = residual - step_size * image_dir
        if iteration + 1 < ITERS:
            precond = precondition(residual)
            image_vec = operate(precond)
            gamma_next, curv_sum = both_sums(residual, precond, image_vec)
            beta_val = gamma_next / gamma_now
            step_size = gamma_next / (curv_sum - beta_val * gamma_next / step_size)
            direction = precond + beta_val * direction
            image_dir = image_vec + beta_val * image_dir
            gamma_now = gamma_next
    return (solution.reshape(1, 1, points, rhs_count), residual.reshape(1, 1, points, rhs_count))


def solution(mesh):
    torus = Mesh(mesh.devices.reshape(8, 2, 2, 2, 4), ("gx_0", "gx_1", "gx_2", "gy_0", "gy_1"))
    return jax.shard_map(
        shards,
        mesh=torus,
        in_specs=(P(GX, GY, None, None), P(GX, GY, None, None), P(GX, GY, None), P(GX, GY, None)),
        out_specs=(P(GX, GY, None, None), P(GX, GY, None, None)),
        check_vma=False,
    )
```

profile of v0, /device:TPU:8, one launch (start us, length us, event | category | flops | bytes accessed | tf_op | source)
XLA Modules:
  0.0 719.8 jit_solution(1988938428017498540)
XLA Ops:
  9.0 4.5 collective-permute-start.6
  35.3 11.7 %cholesky.132 = f32[128,128]{1,0:T(8,128)S(1)} custom-call(f32[128,128]{1,0:T(8,128)S(1)} %cholesky.337), custom_call_target="Cholesky" | custom-call | tf_op jit(solution)/shard_map/jit(cholesky)/cholesky | solution.py:121
  47.2 9.8 %custom-call.38 = f32[1,128,128]{1,2,0:T(8,128)S(1)} custom-call(f32[1,128,128]{2,1,0:T(8,128)S(1)} %get-tuple-element.120), custom_call_target="InvertDiagBlocksLowerTriangular" | custom-call | tf_op jit(solution)/shard_map/jit(cholesky)/cholesky | solution.py:121
  59.6 12.1 %cholesky.270 = f32[128,128]{1,0:T(8,128)S(1)} custom-call(f32[128,128]{1,0:T(8,128)S(1)} %cholesky.341), custom_call_target="Cholesky" | custom-call | tf_op jit(solution)/shard_map/jit(cholesky)/cholesky | solution.py:121
  73.2 9.8 %custom-call.39 = f32[1,128,128]{1,2,0:T(8,128)S(1)} custom-call(f32[1,128,128]{2,1,0:T(8,128)S(1)} %get-tuple-element.117), custom_call_target="InvertDiagBlocksLowerTriangular" | custom-call | tf_op jit(solution)/shard_map/jit(cholesky)/cholesky | solution.py:121
  84.7 11.7 %cholesky.291 = f32[128,128]{1,0:T(8,128)S(1)} custom-call(f32[128,128]{1,0:T(8,128)S(1)} %cholesky.346), custom_call_target="Cholesky" | custom-call | tf_op jit(solution)/shard_map/jit(cholesky)/cholesky | solution.py:121
  97.2 9.8 %custom-call.40 = f32[1,128,128]{1,2,0:T(8,128)S(1)} custom-call(f32[1,128,128]{2,1,0:T(8,128)S(1)} %get-tuple-element.114), custom_call_target="InvertDiagBlocksLowerTriangular" | custom-call | tf_op jit(solution)/shard_map/jit(cholesky)/cholesky | solution.py:121
  108.8 11.7 %cholesky.310 = f32[128,128]{1,0:T(8,128)S(1)} custom-call(f32[128,128]{1,0:T(8,128)S(1)} %cholesky.351), custom_call_target="Cholesky" | custom-call | tf_op jit(solution)/shard_map/jit(cholesky)/cholesky | solution.py:121
  121.3 9.8 %custom-call.41 = f32[1,128,128]{1,2,0:T(8,128)S(1)} custom-call(f32[1,128,128]{2,1,0:T(8,128)S(1)} %get-tuple-element.111), custom_call_target="InvertDiagBlocksLowerTriangular" | custom-call | tf_op jit(solution)/shard_map/jit(cholesky)/cholesky | solution.py:121
  132.5 11.7 %cholesky.327 = f32[128,128]{1,0:T(8,128)S(1)} custom-call(f32[128,128]{1,0:T(8,128)S(1)} %convolution_subtract_fusion.6), custom_call_target="Cholesky" | custom-call | tf_op jit(solution)/shard_map/jit(cholesky)/cholesky | solution.py:121
  149.3 17.9 %while.1 = (s32[]{:T(128)}, f32[640,640]{1,0:T(8,128)}, s32[5,2]{0,1:T(2,128)S(1)}, f32[5,128,128]{2,1,0:T(8,128)}, s32[]{:T(128)}) while((s32[]{:T(128)}, f32[640,640]{1,0:T(8,128)}, s32[5,2]{0,1:T(2,128)S(1)}, f32[5,128,128]{2,1,0:T(8,128)}, s32[]{:T(128)}) %tuple.99), condition=%wide.while_cond, body=%wide.while_body.sunk | while | flops 2 | bytes 132705 | solution.py:122
  167.2 50.1 %custom-call.42 = f32[5,128,128]{1,2,0:T(8,128)S(1)} custom-call(f32[5,128,128]{2,1,0:T(8,128)} %get-tuple-element.10), custom_call_target="InvertDiagBlocksLowerTriangular" | custom-call | tf_op jit(solution)/shard_map/triangular_solve | solution.py:122
  228.6 7.2 %collective-permute-start.11 = (f32[128,256]{1,0:T(8,128)S(1)}, f32[128,256]{1,0:T(8,128)S(1)}, u32[]{:S(2)}, u32[]{:S(2)}) collective-permute-start(f32[128,256]{1,0:T(8,128)S(1)} %get-tuple-element.98), channel_id=1, source_target_pairs={{0,1},{1,2},{2,3},{3,4},{4,5},{5,6},{6,7},{8,9},{9,10},{10,11},{11... | collective-permute-start | bytes 393224 | tf_op jit(solution)/shard_map/ppermute | solution.py:25
  235.9 5.0 fusion.241
  245.8 4.0 collective-permute-done.12
  249.8 7.8 %collective-permute-start.14 = (f32[3,128,256]{2,1,0:T(8,128)S(1)}, f32[3,128,256]{2,1,0:T(8,128)S(1)}, u32[]{:S(2)}, u32[]{:S(2)}) collective-permute-start(f32[3,128,256]{2,1,0:T(8,128)S(1)} %pad_maximum_fusion.5), channel_id=1, source_target_pairs={{0,1},{1,2},{2,3},{3,4},{4,5},{5,6},{6,7},{8,9},{9,10},{10,11},{11... | collective-permute-start | bytes 1179656 | tf_op jit(solution)/shard_map/ppermute | solution.py:25
  259.5 5.3 collective-permute-done.14
  265.5 7.4 %collective-permute-done.15 = f32[3,128,256]{2,1,0:T(8,128)S(1)} collective-permute-done((f32[3,128,256]{2,1,0:T(8,128)S(1)}, f32[3,128,256]{2,1,0:T(8,128)S(1)}, u32[]{:S(2)}, u32[]{:S(2)}) %collective-permute-start.15) | collective-permute-done | bytes 393248 | tf_op jit(solution)/shard_map/ppermute | solution.py:25
  275.4 14.8 %collective-permute-done.16 = f32[512,256]{1,0:T(8,128)S(1)} collective-permute-done((f32[512,256]{1,0:T(8,128)S(1)}, f32[512,256]{1,0:T(8,128)S(1)}, u32[]{:S(2)}, u32[]{:S(2)}) %collective-permute-start.16) | collective-permute-done | bytes 524320 | tf_op jit(solution)/shard_map/ppermute | solution.py:19
  290.4 5.2 collective-permute-start.18
  302.8 22.2 %collective-permute-done.18 = f32[3,512,256]{2,1,0:T(8,128)S(1)} collective-permute-done((f32[3,512,256]{2,1,0:T(8,128)S(1)}, f32[3,512,256]{2,1,0:T(8,128)S(1)}, u32[]{:S(2)}, u32[]{:S(2)}) %collective-permute-start.18) | collective-permute-done | bytes 1572896 | tf_op jit(solution)/shard_map/ppermute | solution.py:25
  337.2 18.6 %all-reduce.3 = (f32[256]{0:T(256)S(1)}, f32[256]{0:T(256)S(1)}) all-reduce(f32[256]{0:T(256)S(1)} %get-tuple-element.16, f32[256]{0:T(256)S(1)} %get-tuple-element.15), channel_id=1, replica_groups=mesh['gx_0'=8,'gx_1'=2,'gx_2'=2,'gy_0'=2,'gy_1'=4] {'gx_0'}, use_global_device_ids=true, to_apply=%region_11.13 | all-reduce | flops 512 | bytes 4096 | tf_op jit(solution)/shard_map/psum | solution.py:30
  355.8 4.9 all-reduce.15
  363.2 18.7 %all-reduce.9 = (f32[256]{0:T(256)S(1)}, f32[256]{0:T(256)S(1)}) all-reduce(f32[256]{0:T(256)S(1)} %get-tuple-element.49, f32[256]{0:T(256)S(1)} %get-tuple-element.50), channel_id=1, replica_groups=mesh['gx_0'=8,'gx_1'=2,'gx_2'=2,'gy_0'=2,'gy_1'=4] {'gy_0'}, use_global_device_ids=true, to_apply=%region_14.16 | all-reduce | flops 512 | bytes 4096 | tf_op jit(solution)/shard_map/psum | solution.py:30
  381.9 10.0 %all-reduce.6 = (f32[256]{0:T(256)S(1)}, f32[256]{0:T(256)S(1)}) all-reduce(f32[256]{0:T(256)S(1)} %get-tuple-element.43, f32[256]{0:T(256)S(1)} %get-tuple-element.44), channel_id=1, replica_groups=mesh['gx_0'=8,'gx_1'=2,'gx_2'=2,'gy_0'=2,'gy_1'=4] {'gy_1'}, use_global_device_ids=true, to_apply=%region_15.17 | all-reduce | flops 512 | bytes 4096 | tf_op jit(solution)/shard_map/psum | solution.py:30
  395.3 8.9 %collective-permute-done.20 = f32[3,128,256]{2,1,0:T(8,128)S(1)} collective-permute-done((f32[3,128,256]{2,1,0:T(8,128)S(1)}, f32[3,128,256]{2,1,0:T(8,128)S(1)}, u32[]{:S(2)}, u32[]{:S(2)}) %collective-permute-start.20) | collective-permute-done | bytes 393248 | tf_op jit(solution)/shard_map/ppermute | solution.py:19
  406.5 5.0 collective-permute-start.23
  417.2 3.6 collective-permute-done.24
  420.8 4.4 collective-permute-start.26
  427.1 5.1 collective-permute-done.26
  432.8 3.5 collective-permute-done.27
  440.1 14.4 %collective-permute-done.28 = f32[512,256]{1,0:T(8,128)S(1)} collective-permute-done((f32[512,256]{1,0:T(8,128)S(1)}, f32[512,256]{1,0:T(8,128)S(1)}, u32[]{:S(2)}, u32[]{:S(2)}) %collective-permute-start.28) | collective-permute-done | bytes 524320 | tf_op jit(solution)/shard_map/ppermute | solution.py:19
  463.0 21.2 %collective-permute-done.30 = f32[3,512,256]{2,1,0:T(8,128)S(1)} collective-permute-done((f32[3,512,256]{2,1,0:T(8,128)S(1)}, f32[3,512,256]{2,1,0:T(8,128)S(1)}, u32[]{:S(2)}, u32[]{:S(2)}) %collective-permute-start.30) | collective-permute-done | bytes 1572896 | tf_op jit(solution)/shard_map/ppermute | solution.py:25
  497.3 19.1 %all-reduce.2 = (f32[256]{0:T(256)S(1)}, f32[256]{0:T(256)S(1)}) all-reduce(f32[256]{0:T(256)S(1)} %get-tuple-element.14, f32[256]{0:T(256)S(1)} %get-tuple-element.13), channel_id=1, replica_groups=mesh['gx_0'=8,'gx_1'=2,'gx_2'=2,'gy_0'=2,'gy_1'=4] {'gx_0'}, use_global_device_ids=true, to_apply=%region_23.25 | all-reduce | flops 512 | bytes 4096 | tf_op jit(solution)/shard_map/psum | solution.py:30
  516.5 4.9 all-reduce.14
  523.8 16.4 %all-reduce.8 = (f32[256]{0:T(256)S(1)}, f32[256]{0:T(256)S(1)}) all-reduce(f32[256]{0:T(256)S(1)} %get-tuple-element.47, f32[256]{0:T(256)S(1)} %get-tuple-element.48), channel_id=1, replica_groups=mesh['gx_0'=8,'gx_1'=2,'gx_2'=2,'gy_0'=2,'gy_1'=4] {'gy_0'}, use_global_device_ids=true, to_apply=%region_26.28 | all-reduce | flops 512 | bytes 4096 | tf_op jit(solution)/shard_map/psum | solution.py:30
  540.3 11.2 %all-reduce.5 = (f32[256]{0:T(256)S(1)}, f32[256]{0:T(256)S(1)}) all-reduce(f32[256]{0:T(256)S(1)} %get-tuple-element.41, f32[256]{0:T(256)S(1)} %get-tuple-element.42), channel_id=1, replica_groups=mesh['gx_0'=8,'gx_1'=2,'gx_2'=2,'gy_0'=2,'gy_1'=4] {'gy_1'}, use_global_device_ids=true, to_apply=%region_27.29 | all-reduce | flops 512 | bytes 4096 | tf_op jit(solution)/shard_map/psum | solution.py:30
  555.9 8.9 %collective-permute-done.32 = f32[3,128,256]{2,1,0:T(8,128)S(1)} collective-permute-done((f32[3,128,256]{2,1,0:T(8,128)S(1)}, f32[3,128,256]{2,1,0:T(8,128)S(1)}, u32[]{:S(2)}, u32[]{:S(2)}) %collective-permute-start.32) | collective-permute-done | bytes 393248 | tf_op jit(solution)/shard_map/ppermute | solution.py:19
  568.6 5.0 collective-permute-start.35
  583.0 4.4 collective-permute-start.38
  589.3 7.5 %collective-permute-done.38 = f32[3,128,256]{2,1,0:T(8,128)S(1)} collective-permute-done((f32[3,128,256]{2,1,0:T(8,128)S(1)}, f32[3,128,256]{2,1,0:T(8,128)S(1)}, u32[]{:S(2)}, u32[]{:S(2)}) %collective-permute-start.38) | collective-permute-done | bytes 393248 | tf_op jit(solution)/shard_map/ppermute | solution.py:25
  597.4 3.6 collective-permute-done.39
  603.5 12.6 %collective-permute-done.40 = f32[512,256]{1,0:T(8,128)S(1)} collective-permute-done((f32[512,256]{1,0:T(8,128)S(1)}, f32[512,256]{1,0:T(8,128)S(1)}, u32[]{:S(2)}, u32[]{:S(2)}) %collective-permute-start.40) | collective-permute-done | bytes 524320 | tf_op jit(solution)/shard_map/ppermute | solution.py:19
  625.6 23.0 %collective-permute-done.42 = f32[3,512,256]{2,1,0:T(8,128)S(1)} collective-permute-done((f32[3,512,256]{2,1,0:T(8,128)S(1)}, f32[3,512,256]{2,1,0:T(8,128)S(1)}, u32[]{:S(2)}, u32[]{:S(2)}) %collective-permute-start.42) | collective-permute-done | bytes 1572896 | tf_op jit(solution)/shard_map/ppermute | solution.py:25
  663.8 17.0 %all-reduce.1 = (f32[256]{0:T(256)S(1)}, f32[256]{0:T(256)S(1)}) all-reduce(f32[256]{0:T(256)S(1)} %get-tuple-element.12, f32[256]{0:T(256)S(1)} %get-tuple-element.11), channel_id=1, replica_groups=mesh['gx_0'=8,'gx_1'=2,'gx_2'=2,'gy_0'=2,'gy_1'=4] {'gx_0'}, use_global_device_ids=true, to_apply=%region_35.37 | all-reduce | flops 512 | bytes 4096 | tf_op jit(solution)/shard_map/psum | solution.py:30
  680.7 4.9 all-reduce.13
  688.1 19.2 %all-reduce.7 = (f32[256]{0:T(256)S(1)}, f32[256]{0:T(256)S(1)}) all-reduce(f32[256]{0:T(256)S(1)} %get-tuple-element.45, f32[256]{0:T(256)S(1)} %get-tuple-element.46), channel_id=1, replica_groups=mesh['gx_0'=8,'gx_1'=2,'gx_2'=2,'gy_0'=2,'gy_1'=4] {'gy_0'}, use_global_device_ids=true, to_apply=%region_38.40 | all-reduce | flops 512 | bytes 4096 | tf_op jit(solution)/shard_map/psum | solution.py:30
  707.3 10.0 %all-reduce.4 = (f32[256]{0:T(256)S(1)}, f32[256]{0:T(256)S(1)}) all-reduce(f32[256]{0:T(256)S(1)} %get-tuple-element.39, f32[256]{0:T(256)S(1)} %get-tuple-element.40), channel_id=1, replica_groups=mesh['gx_0'=8,'gx_1'=2,'gx_2'=2,'gy_0'=2,'gy_1'=4] {'gy_1'}, use_global_device_ids=true, to_apply=%region_39.41 | all-reduce | flops 512 | bytes 4096 | tf_op jit(solution)/shard_map/psum | solution.py:30
  (301 shorter events, 196.5 us)
Async XLA Ops:
  0.7 6.9 collective-permute-start.4
  0.7 6.8 collective-permute-start.5
  3.2 16.9 %collective-permute-start = (f32[3,512]{1,0:T(4,128)S(1)}, f32[3,512]{1,0:T(4,128)S(1)}, u32[]{:S(2)}, u32[]{:S(2)}) collective-permute-start(f32[3,512]{1,0:T(4,128)S(1)} %get-tuple-element.147), channel_id=1, source_target_pairs={{0,8},{8,16},{16,24},{24,32},{32,40},{40,48},{48,56},{56,64},{64,7... | collective-permute-start | bytes 18440 | tf_op jit(solution)/shard_map/ppermute | solution.py:19
  3.4 16.6 %collective-permute-start.1 = (f32[3,512]{1,0:T(4,128)S(1)}, f32[3,512]{1,0:T(4,128)S(1)}, u32[]{:S(2)}, u32[]{:S(2)}) collective-permute-start(f32[3,512]{1,0:T(4,128)S(1)} %get-tuple-element.147), channel_id=1, source_target_pairs={{0,248},{8,0},{16,8},{24,16},{32,24},{40,32},{48,40},{56,48},{64,5... | collective-permute-start | bytes 18440 | tf_op jit(solution)/shard_map/ppermute | solution.py:19
  7.7 6.7 collective-permute-start.7
  9.0 6.3 collective-permute-start.6
  17.1 209.0 %collective-permute-start.8 = (f32[3,128,256]{2,1,0:T(8,128)}, f32[3,128,256]{2,1,0:T(8,128)}, u32[]{:S(2)}, u32[]{:S(2)}) collective-permute-start(f32[3,128,256]{2,1,0:T(8,128)} %pad_maximum_fusion.3), channel_id=1, source_target_pairs={{0,248},{8,0},{16,8},{24,16},{32,24},{40,32},{48,40},{56,48},{64,5... | collective-permute-start | bytes 1179656 | tf_op jit(solution)/shard_map/ppermute | solution.py:19
  20.1 6.6 collective-permute-start.2
  23.5 5.7 collective-permute-start.3
  25.6 200.5 %collective-permute-start.9 = (f32[3,128,256]{2,1,0:T(8,128)}, f32[3,128,256]{2,1,0:T(8,128)}, u32[]{:S(2)}, u32[]{:S(2)}) collective-permute-start(f32[3,128,256]{2,1,0:T(8,128)} %pad_maximum_fusion.4), channel_id=1, source_target_pairs={{0,8},{8,16},{16,24},{24,32},{32,40},{40,48},{48,56},{56,64},{64,7... | collective-permute-start | bytes 1179656 | tf_op jit(solution)/shard_map/ppermute | solution.py:19
  227.3 13.6 %collective-permute-start.10 = (f32[128,256]{1,0:T(8,128)S(1)}, f32[128,256]{1,0:T(8,128)S(1)}, u32[]{:S(2)}, u32[]{:S(2)}) collective-permute-start(f32[128,256]{1,0:T(8,128)S(1)} %get-tuple-element.97), channel_id=1, source_target_pairs={{1,0},{2,1},{3,2},{4,3},{5,4},{6,5},{7,6},{9,8},{10,9},{11,10},{12... | collective-permute-start | bytes 393224 | tf_op jit(solution)/shard_map/ppermute | solution.py:25
  228.6 12.3 %collective-permute-start.11 = (f32[128,256]{1,0:T(8,128)S(1)}, f32[128,256]{1,0:T(8,128)S(1)}, u32[]{:S(2)}, u32[]{:S(2)}) collective-permute-start(f32[128,256]{1,0:T(8,128)S(1)} %get-tuple-element.98), channel_id=1, source_target_pairs={{0,1},{1,2},{2,3},{3,4},{4,5},{5,6},{6,7},{8,9},{9,10},{10,11},{11... | collective-permute-start | bytes 393224 | tf_op jit(solution)/shard_map/ppermute | solution.py:25
  242.8 7.0 collective-permute-start.12
  242.8 6.9 collective-permute-start.13
  249.8 15.0 %collective-permute-start.14 = (f32[3,128,256]{2,1,0:T(8,128)S(1)}, f32[3,128,256]{2,1,0:T(8,128)S(1)}, u32[]{:S(2)}, u32[]{:S(2)}) collective-permute-start(f32[3,128,256]{2,1,0:T(8,128)S(1)} %pad_maximum_fusion.5), channel_id=1, source_target_pairs={{0,1},{1,2},{2,3},{3,4},{4,5},{5,6},{6,7},{8,9},{9,10},{10,11},{11... | collective-permute-start | bytes 1179656 | tf_op jit(solution)/shard_map/ppermute | solution.py:25
  257.6 15.3 %collective-permute-start.15 = (f32[3,128,256]{2,1,0:T(8,128)S(1)}, f32[3,128,256]{2,1,0:T(8,128)S(1)}, u32[]{:S(2)}, u32[]{:S(2)}) collective-permute-start(f32[3,128,256]{2,1,0:T(8,128)S(1)} %pad_maximum_fusion.5), channel_id=1, source_target_pairs={{1,0},{2,1},{3,2},{4,3},{5,4},{6,5},{7,6},{9,8},{10,9},{11,10},{12... | collective-permute-start | bytes 1179656 | tf_op jit(solution)/shard_map/ppermute | solution.py:25
  273.5 61.6 %copy-start.1 = (f32[512,256]{1,0:T(8,128)}, f32[512,256]{1,0:T(8,128)S(1)}, u32[]{:S(2)}) copy-start(f32[512,256]{1,0:T(8,128)S(1)} %convolution_add_fusion.5) | copy-start | bytes 1572868
  273.6 16.7 %collective-permute-start.16 = (f32[512,256]{1,0:T(8,128)S(1)}, f32[512,256]{1,0:T(8,128)S(1)}, u32[]{:S(2)}, u32[]{:S(2)}) collective-permute-start(f32[512,256]{1,0:T(8,128)S(1)} %convolution_add_fusion.5), channel_id=1, source_target_pairs={{0,8},{8,16},{16,24},{24,32},{32,40},{40,48},{48,56},{56,64},{64,7... | collective-permute-start | bytes 1572872 | tf_op jit(solution)/shard_map/ppermute | solution.py:19
  273.7 16.6 %collective-permute-start.17 = (f32[512,256]{1,0:T(8,128)S(1)}, f32[512,256]{1,0:T(8,128)S(1)}, u32[]{:S(2)}, u32[]{:S(2)}) collective-permute-start(f32[512,256]{1,0:T(8,128)S(1)} %convolution_add_fusion.5), channel_id=1, source_target_pairs={{0,248},{8,0},{16,8},{24,16},{32,24},{40,32},{48,40},{56,48},{64,5... | collective-permute-start | bytes 1572872 | tf_op jit(solution)/shard_map/ppermute | solution.py:19
  290.4 34.6 %collective-permute-start.18 = (f32[3,512,256]{2,1,0:T(8,128)S(1)}, f32[3,512,256]{2,1,0:T(8,128)S(1)}, u32[]{:S(2)}, u32[]{:S(2)}) collective-permute-start(f32[3,512,256]{2,1,0:T(8,128)S(1)} %pad_maximum_fusion), channel_id=1, source_target_pairs={{0,1},{1,2},{2,3},{3,4},{4,5},{5,6},{6,7},{8,9},{9,10},{10,11},{11... | collective-permute-start | bytes 4718600 | tf_op jit(solution)/shard_map/ppermute | solution.py:25
  295.7 35.4 %collective-permute-start.19 = (f32[3,512,256]{2,1,0:T(8,128)S(1)}, f32[3,512,256]{2,1,0:T(8,128)S(1)}, u32[]{:S(2)}, u32[]{:S(2)}) collective-permute-start(f32[3,512,256]{2,1,0:T(8,128)S(1)} %pad_maximum_fusion), channel_id=1, source_target_pairs={{1,0},{2,1},{3,2},{4,3},{5,4},{6,5},{7,6},{9,8},{10,9},{11,10},{12... | collective-permute-start | bytes 4718600 | tf_op jit(solution)/shard_map/ppermute | solution.py:25
  394.6 9.6 %collective-permute-start.20 = (f32[3,128,256]{2,1,0:T(8,128)S(1)}, f32[3,128,256]{2,1,0:T(8,128)S(1)}, u32[]{:S(2)}, u32[]{:S(2)}) collective-permute-start(f32[3,128,256]{2,1,0:T(8,128)S(1)} %pad_maximum_fusion.6), channel_id=1, source_target_pairs={{0,248},{8,0},{16,8},{24,16},{32,24},{40,32},{48,40},{56,48},{64,5... | collective-permute-start | bytes 1179656 | tf_op jit(solution)/shard_map/ppermute | solution.py:19
  394.7 10.4 %collective-permute-start.21 = (f32[3,128,256]{2,1,0:T(8,128)S(1)}, f32[3,128,256]{2,1,0:T(8,128)S(1)}, u32[]{:S(2)}, u32[]{:S(2)}) collective-permute-start(f32[3,128,256]{2,1,0:T(8,128)S(1)} %pad_maximum_fusion.7), channel_id=1, source_target_pairs={{0,8},{8,16},{16,24},{24,32},{32,40},{40,48},{48,56},{56,64},{64,7... | collective-permute-start | bytes 1179656 | tf_op jit(solution)/shard_map/ppermute | solution.py:19
  405.2 6.9 collective-permute-start.22
  406.5 7.1 collective-permute-start.23
  415.3 5.4 collective-permute-start.24
  415.4 5.3 collective-permute-start.25
  420.8 11.4 %collective-permute-start.26 = (f32[3,128,256]{2,1,0:T(8,128)S(1)}, f32[3,128,256]{2,1,0:T(8,128)S(1)}, u32[]{:S(2)}, u32[]{:S(2)}) collective-permute-start(f32[3,128,256]{2,1,0:T(8,128)S(1)} %pad_maximum_fusion.8), channel_id=1, source_target_pairs={{0,1},{1,2},{2,3},{3,4},{4,5},{5,6},{6,7},{8,9},{9,10},{10,11},{11... | collective-permute-start | bytes 1179656 | tf_op jit(solution)/shard_map/ppermute | solution.py:25
  425.2 11.1 %collective-permute-start.27 = (f32[3,128,256]{2,1,0:T(8,128)S(1)}, f32[3,128,256]{2,1,0:T(8,128)S(1)}, u32[]{:S(2)}, u32[]{:S(2)}) collective-permute-start(f32[3,128,256]{2,1,0:T(8,128)S(1)} %pad_maximum_fusion.8), channel_id=1, source_target_pairs={{1,0},{2,1},{3,2},{4,3},{5,4},{6,5},{7,6},{9,8},{10,9},{11,10},{12... | collective-permute-start | bytes 1179656 | tf_op jit(solution)/shard_map/ppermute | solution.py:25
  437.0 57.5 %copy-start.3 = (f32[512,256]{1,0:T(8,128)}, f32[512,256]{1,0:T(8,128)S(1)}, u32[]{:S(2)}) copy-start(f32[512,256]{1,0:T(8,128)S(1)} %convolution_add_fusion.4) | copy-start | bytes 1572868
  437.0 17.5 %collective-permute-start.28 = (f32[512,256]{1,0:T(8,128)S(1)}, f32[512,256]{1,0:T(8,128)S(1)}, u32[]{:S(2)}, u32[]{:S(2)}) collective-permute-start(f32[512,256]{1,0:T(8,128)S(1)} %convolution_add_fusion.4), channel_id=1, source_target_pairs={{0,8},{8,16},{16,24},{24,32},{32,40},{40,48},{48,56},{56,64},{64,7... | collective-permute-start | bytes 1572872 | tf_op jit(solution)/shard_map/ppermute | solution.py:19
  437.1 17.4 %collective-permute-start.29 = (f32[512,256]{1,0:T(8,128)S(1)}, f32[512,256]{1,0:T(8,128)S(1)}, u32[]{:S(2)}, u32[]{:S(2)}) collective-permute-start(f32[512,256]{1,0:T(8,128)S(1)} %convolution_add_fusion.4), channel_id=1, source_target_pairs={{0,248},{8,0},{16,8},{24,16},{32,24},{40,32},{48,40},{56,48},{64,5... | collective-permute-start | bytes 1572872 | tf_op jit(solution)/shard_map/ppermute | solution.py:19
  454.6 29.7 %collective-permute-start.30 = (f32[3,512,256]{2,1,0:T(8,128)S(1)}, f32[3,512,256]{2,1,0:T(8,128)S(1)}, u32[]{:S(2)}, u32[]{:S(2)}) collective-permute-start(f32[3,512,256]{2,1,0:T(8,128)S(1)} %pad_maximum_fusion.1), channel_id=1, source_target_pairs={{0,1},{1,2},{2,3},{3,4},{4,5},{5,6},{6,7},{8,9},{9,10},{10,11},{11... | collective-permute-start | bytes 4718600 | tf_op jit(solution)/shard_map/ppermute | solution.py:25
  456.0 34.5 %collective-permute-start.31 = (f32[3,512,256]{2,1,0:T(8,128)S(1)}, f32[3,512,256]{2,1,0:T(8,128)S(1)}, u32[]{:S(2)}, u32[]{:S(2)}) collective-permute-start(f32[3,512,256]{2,1,0:T(8,128)S(1)} %pad_maximum_fusion.1), channel_id=1, source_target_pairs={{1,0},{2,1},{3,2},{4,3},{5,4},{6,5},{7,6},{9,8},{10,9},{11,10},{12... | collective-permute-start | bytes 4718600 | tf_op jit(solution)/shard_map/ppermute | solution.py:25
  555.2 9.6 %collective-permute-start.32 = (f32[3,128,256]{2,1,0:T(8,128)S(1)}, f32[3,128,256]{2,1,0:T(8,128)S(1)}, u32[]{:S(2)}, u32[]{:S(2)}) collective-permute-start(f32[3,128,256]{2,1,0:T(8,128)S(1)} %pad_maximum_fusion.9), channel_id=1, source_target_pairs={{0,248},{8,0},{16,8},{24,16},{32,24},{40,32},{48,40},{56,48},{64,5... | collective-permute-start | bytes 1179656 | tf_op jit(solution)/shard_map/ppermute | solution.py:19
  555.3 11.9 %collective-permute-start.33 = (f32[3,128,256]{2,1,0:T(8,128)S(1)}, f32[3,128,256]{2,1,0:T(8,128)S(1)}, u32[]{:S(2)}, u32[]{:S(2)}) collective-permute-start(f32[3,128,256]{2,1,0:T(8,128)S(1)} %pad_maximum_fusion.10), channel_id=1, source_target_pairs={{0,8},{8,16},{16,24},{24,32},{32,40},{40,48},{48,56},{56,64},{64,7... | collective-permute-start | bytes 1179656 | tf_op jit(solution)/shard_map/ppermute | solution.py:19
  567.3 6.9 collective-permute-start.34
  568.6 7.1 collective-permute-start.35
  577.4 4.5 collective-permute-start.36
  577.5 5.4 collective-permute-start.37
  583.0 13.8 %collective-permute-start.38 = (f32[3,128,256]{2,1,0:T(8,128)S(1)}, f32[3,128,256]{2,1,0:T(8,128)S(1)}, u32[]{:S(2)}, u32[]{:S(2)}) collective-permute-start(f32[3,128,256]{2,1,0:T(8,128)S(1)} %pad_maximum_fusion.11), channel_id=1, source_target_pairs={{0,1},{1,2},{2,3},{3,4},{4,5},{5,6},{6,7},{8,9},{9,10},{10,11},{11... | collective-permute-start | bytes 1179656 | tf_op jit(solution)/shard_map/ppermute | solution.py:25
  587.4 13.6 %collective-permute-start.39 = (f32[3,128,256]{2,1,0:T(8,128)S(1)}, f32[3,128,256]{2,1,0:T(8,128)S(1)}, u32[]{:S(2)}, u32[]{:S(2)}) collective-permute-start(f32[3,128,256]{2,1,0:T(8,128)S(1)} %pad_maximum_fusion.11), channel_id=1, source_target_pairs={{1,0},{2,1},{3,2},{4,3},{5,4},{6,5},{7,6},{9,8},{10,9},{11,10},{12... | collective-permute-start | bytes 1179656 | tf_op jit(solution)/shard_map/ppermute | solution.py:25
  601.7 14.4 %collective-permute-start.40 = (f32[512,256]{1,0:T(8,128)S(1)}, f32[512,256]{1,0:T(8,128)S(1)}, u32[]{:S(2)}, u32[]{:S(2)}) collective-permute-start(f32[512,256]{1,0:T(8,128)S(1)} %convolution_add_fusion.3), channel_id=1, source_target_pairs={{0,8},{8,16},{16,24},{24,32},{32,40},{40,48},{48,56},{56,64},{64,7... | collective-permute-start | bytes 1572872 | tf_op jit(solution)/shard_map/ppermute | solution.py:19
  601.8 14.4 %collective-permute-start.41 = (f32[512,256]{1,0:T(8,128)S(1)}, f32[512,256]{1,0:T(8,128)S(1)}, u32[]{:S(2)}, u32[]{:S(2)}) collective-permute-start(f32[512,256]{1,0:T(8,128)S(1)} %convolution_add_fusion.3), channel_id=1, source_target_pairs={{0,248},{8,0},{16,8},{24,16},{32,24},{40,32},{48,40},{56,48},{64,5... | collective-permute-start | bytes 1572872 | tf_op jit(solution)/shard_map/ppermute | solution.py:19
  616.2 32.4 %collective-permute-start.42 = (f32[3,512,256]{2,1,0:T(8,128)S(1)}, f32[3,512,256]{2,1,0:T(8,128)S(1)}, u32[]{:S(2)}, u32[]{:S(2)}) collective-permute-start(f32[3,512,256]{2,1,0:T(8,128)S(1)} %pad_maximum_fusion.2), channel_id=1, source_target_pairs={{0,1},{1,2},{2,3},{3,4},{4,5},{5,6},{6,7},{8,9},{9,10},{10,11},{11... | collective-permute-start | bytes 4718600 | tf_op jit(solution)/shard_map/ppermute | solution.py:25
  618.6 38.4 %collective-permute-start.43 = (f32[3,512,256]{2,1,0:T(8,128)S(1)}, f32[3,512,256]{2,1,0:T(8,128)S(1)}, u32[]{:S(2)}, u32[]{:S(2)}) collective-permute-start(f32[3,512,256]{2,1,0:T(8,128)S(1)} %pad_maximum_fusion.2), channel_id=1, source_target_pairs={{1,0},{2,1},{3,2},{4,3},{5,4},{6,5},{7,6},{9,8},{10,9},{11,10},{12... | collective-permute-start | bytes 4718600 | tf_op jit(solution)/shard_map/ppermute | solution.py:25
  660.8 56.5 %copy-start.2 = (f32[512,256]{1,0:T(8,128)S(1)}, f32[512,256]{1,0:T(8,128)}, u32[]{:S(2)}) copy-start(f32[512,256]{1,0:T(8,128)} %copy-done.1) | copy-start | bytes 1572868
  660.8 56.4 %copy-start.4 = (f32[512,256]{1,0:T(8,128)S(1)}, f32[512,256]{1,0:T(8,128)}, u32[]{:S(2)}) copy-start(f32[512,256]{1,0:T(8,128)} %copy-done.3) | copy-start | bytes 1572868
  (25 other events, 361.8 us)
where the time goes:
time: 727 us; the launch traced here: 720 us
  waiting for transfers between devices  183 us (25%)
  other arithmetic  167 us (23%)
  blocking collectives  162 us (22%)
  matrix products  92.3 us (13%)
  starting transfers between devices  86.8 us (12%)
  local copies, waits for them, and re-layouts  23.7 us (3%)
    psum x15, blocking collectives, over_axes(): value = lax.psum(value, axis)  162 us
    ppermute x22, waiting for transfers between devices, passed_along(): return lax.ppermute(block, axis, route)  108 us
    another operation x19, other arithmetic, shards(): factor = jnp.linalg.cholesky(local_matrix)  102 us
    ppermute x22, waiting for transfers between devices, shifted(): lax.ppermute(value, axis, [(i, (i + by) % count) for i in range(count)])  74.3 us
    ppermute x22, starting transfers between devices, passed_along(): return lax.ppermute(block, axis, route)  65.3 us
    dot_general x27, matrix products, operate(): jnp.dot(kernel_block(own_pos, positions[row_off][col_off]), columns[col_o...  52.9 us
    another operation x3, other arithmetic, shards(): lax.linalg.triangular_solve(factor, jnp.eye(ext_len, dtype=jnp.float32),...  51.4 us
    ppermute x22, starting transfers between devices, shifted(): lax.ppermute(value, axis, [(i, (i + by) % count) for i in range(count)])  21.5 us
  transfers between devices with their start and end apart: 44, of which 28 were waited for; matrix products, arithmetic and copies ran while one was open for 34% of the time, Pallas kernels for 0%

commit v1 on v0

--- a/solution.py
+++ b/solution.py
@@ -27,7 +27,8 @@
 
 def over_axes(value, axes):
     for axis in axes:
-        value = lax.psum(value, axis)
+        value_now = jax.lax.all_gather(value, axis_name=axis)
+        value = jnp.sum(value_now, axis=0)
     return value
 
 

time: 727 us -> 815 us (1.12)
  blocking collectives: 162 us -> 246 us
    all_gather x0 -> x30, blocking collectives: none -> 246 us  [over_axes(): value_now = jax.lax.all_gather(value, axis_name=axis)]
    psum x15 -> x0, blocking collectives: 162 us -> none  [over_axes(): value = lax.psum(value, axis)]
  transfers between devices with their start and end apart: 44 -> 44, of which waited for: 28 -> 27; matrix products, arithmetic and copies ran while one was open for 34% -> 30% of each run, Pallas kernels for 0% -> 0%
where the time goes in v1:
time: 815 us; the launch traced here: 806 us
  blocking collectives  246 us (30%)
  waiting for transfers between devices  187 us (23%)
  other arithmetic  167 us (20%)
  matrix products  92.3 us (11%)
  starting transfers between devices  83.8 us (10%)
  local copies, waits for them, and re-layouts  23.5 us (3%)
    all_gather x30, blocking collectives, over_axes(): value_now = jax.lax.all_gather(value, axis_name=axis)  246 us
    ppermute x22, waiting for transfers between devices, passed_along(): return lax.ppermute(block, axis, route)  105 us
    another operation x19, other arithmetic, shards(): factor = jnp.linalg.cholesky(local_matrix)  102 us
    ppermute x22, waiting for transfers between devices, shifted(): lax.ppermute(value, axis, [(i, (i + by) % count) for i in range(count)])  82.2 us
    ppermute x22, starting transfers between devices, passed_along(): return lax.ppermute(block, axis, route)  61.7 us
    dot_general x27, matrix products, operate(): jnp.dot(kernel_block(own_pos, positions[row_off][col_off]), columns[col_o...  52.9 us
    another operation x3, other arithmetic, shards(): lax.linalg.triangular_solve(factor, jnp.eye(ext_len, dtype=jnp.float32),...  51.4 us
    ppermute x22, starting transfers between devices, shifted(): lax.ppermute(value, axis, [(i, (i + by) % count) for i in range(count)])  22.1 us
  transfers between devices with their start and end apart: 44, of which 27 were waited for; matrix products, arithmetic and copies ran while one was open for 30% of the time, Pallas kernels for 0%

profile of v1, /device:TPU:8, one launch (start us, length us, event | category | flops | bytes accessed | tf_op | source)
XLA Modules:
  0.0 805.9 jit_solution(7705376196644096273)
XLA Ops:
  35.3 11.7 %cholesky.132 = f32[128,128]{1,0:T(8,128)S(1)} custom-call(f32[128,128]{1,0:T(8,128)S(1)} %cholesky.337), custom_call_target="Cholesky" | custom-call | tf_op jit(solution)/shard_map/jit(cholesky)/cholesky | solution.py:122
  47.1 9.8 %custom-call.38 = f32[1,128,128]{1,2,0:T(8,128)S(1)} custom-call(f32[1,128,128]{2,1,0:T(8,128)S(1)} %get-tuple-element.90), custom_call_target="InvertDiagBlocksLowerTriangular" | custom-call | tf_op jit(solution)/shard_map/jit(cholesky)/cholesky | solution.py:122
  59.6 12.1 %cholesky.270 = f32[128,128]{1,0:T(8,128)S(1)} custom-call(f32[128,128]{1,0:T(8,128)S(1)} %cholesky.341), custom_call_target="Cholesky" | custom-call | tf_op jit(solution)/shard_map/jit(cholesky)/cholesky | solution.py:122
  73.1 9.8 %custom-call.39 = f32[1,128,128]{1,2,0:T(8,128)S(1)} custom-call(f32[1,128,128]{2,1,0:T(8,128)S(1)} %get-tuple-element.87), custom_call_target="InvertDiagBlocksLowerTriangular" | custom-call | tf_op jit(solution)/shard_map/jit(cholesky)/cholesky | solution.py:122
  84.7 11.7 %cholesky.291 = f32[128,128]{1,0:T(8,128)S(1)} custom-call(f32[128,128]{1,0:T(8,128)S(1)} %cholesky.346), custom_call_target="Cholesky" | custom-call | tf_op jit(solution)/shard_map/jit(cholesky)/cholesky | solution.py:122
  97.1 9.8 %custom-call.40 = f32[1,128,128]{1,2,0:T(8,128)S(1)} custom-call(f32[1,128,128]{2,1,0:T(8,128)S(1)} %get-tuple-element.84), custom_call_target="InvertDiagBlocksLowerTriangular" | custom-call | tf_op jit(solution)/shard_map/jit(cholesky)/cholesky | solution.py:122
  108.8 11.7 %cholesky.310 = f32[128,128]{1,0:T(8,128)S(1)} custom-call(f32[128,128]{1,0:T(8,128)S(1)} %cholesky.351), custom_call_target="Cholesky" | custom-call | tf_op jit(solution)/shard_map/jit(cholesky)/cholesky | solution.py:122
  121.2 9.8 %custom-call.41 = f32[1,128,128]{1,2,0:T(8,128)S(1)} custom-call(f32[1,128,128]{2,1,0:T(8,128)S(1)} %get-tuple-element.81), custom_call_target="InvertDiagBlocksLowerTriangular" | custom-call | tf_op jit(solution)/shard_map/jit(cholesky)/cholesky | solution.py:122
  132.5 11.7 %cholesky.327 = f32[128,128]{1,0:T(8,128)S(1)} custom-call(f32[128,128]{1,0:T(8,128)S(1)} %convolution_subtract_fusion.6), custom_call_target="Cholesky" | custom-call | tf_op jit(solution)/shard_map/jit(cholesky)/cholesky | solution.py:122
  149.2 17.7 %while.1 = (s32[]{:T(128)}, f32[640,640]{1,0:T(8,128)}, s32[5,2]{0,1:T(2,128)S(1)}, f32[5,128,128]{2,1,0:T(8,128)}, s32[]{:T(128)}) while((s32[]{:T(128)}, f32[640,640]{1,0:T(8,128)}, s32[5,2]{0,1:T(2,128)S(1)}, f32[5,128,128]{2,1,0:T(8,128)}, s32[]{:T(128)}) %tuple.99), condition=%wide.while_cond, body=%wide.while_body.sunk | while | flops 2 | bytes 132705 | solution.py:123
  166.9 50.1 %custom-call.42 = f32[5,128,128]{1,2,0:T(8,128)S(1)} custom-call(f32[5,128,128]{2,1,0:T(8,128)} %get-tuple-element.10), custom_call_target="InvertDiagBlocksLowerTriangular" | custom-call | tf_op jit(solution)/shard_map/triangular_solve | solution.py:123
  228.4 7.2 collective-permute-start.11
  235.6 5.0 fusion.241
  249.6 7.8 collective-permute-start.14
  259.3 5.3 collective-permute-done.14
  265.2 7.4 collective-permute-done.15
  275.2 14.8 %collective-permute-done.16 = f32[512,256]{1,0:T(8,128)S(1)} collective-permute-done((f32[512,256]{1,0:T(8,128)S(1)}, f32[512,256]{1,0:T(8,128)S(1)}, u32[]{:S(2)}, u32[]{:S(2)}) %collective-permute-start.16) | collective-permute-done | bytes 524320 | tf_op jit(solution)/shard_map/ppermute | solution.py:19
  290.1 5.2 collective-permute-start.18
  302.5 22.2 %collective-permute-done.18 = f32[3,512,256]{2,1,0:T(8,128)S(1)} collective-permute-done((f32[3,512,256]{2,1,0:T(8,128)S(1)}, f32[3,512,256]{2,1,0:T(8,128)S(1)}, u32[]{:S(2)}, u32[]{:S(2)}) %collective-permute-start.18) | collective-permute-done | bytes 1572896 | tf_op jit(solution)/shard_map/ppermute | solution.py:25
  336.9 17.8 %all-gather.30 = f32[8,1,256]{2,1,0:T(1,128)S(1)} all-gather(f32[1,1,256]{2,1,0:T(1,128)S(1)} %bitcast.548), channel_id=2, replica_groups=mesh['gx_0'=8,'gx_1'=2,'gx_2'=2,'gy_0'=2,'gy_1'=4] {'gx_0'}, dimensions={0}, use_global_device_ids=true | all-gather | bytes 9216 | tf_op jit(solution)/shard_map/all_gather | solution.py:30
  360.8 18.0 %all-gather.33 = f32[2,1,256]{2,1,0:T(1,128)S(1)} all-gather(f32[1,1,256]{2,1,0:T(1,128)S(1)} %bitcast.414), channel_id=5, replica_groups=mesh['gx_0'=8,'gx_1'=2,'gx_2'=2,'gy_0'=2,'gy_1'=4] {'gy_0'}, dimensions={0}, use_global_device_ids=true | all-gather | bytes 3072 | tf_op jit(solution)/shard_map/all_gather | solution.py:30
  378.8 9.3 %all-gather.34 = f32[4,1,256]{2,1,0:T(1,128)S(1)} all-gather(f32[1,1,256]{2,1,0:T(1,128)S(1)} %bitcast.415), channel_id=6, replica_groups=mesh['gx_0'=8,'gx_1'=2,'gx_2'=2,'gy_0'=2,'gy_1'=4] {'gy_1'}, dimensions={0}, use_global_device_ids=true | all-gather | bytes 5120 | tf_op jit(solution)/shard_map/all_gather | solution.py:30
  388.2 14.4 %all-gather.35 = f32[8,1,256]{2,1,0:T(1,128)S(1)} all-gather(f32[1,1,256]{2,1,0:T(1,128)S(1)} %bitcast.545), channel_id=7, replica_groups=mesh['gx_0'=8,'gx_1'=2,'gx_2'=2,'gy_0'=2,'gy_1'=4] {'gx_0'}, dimensions={0}, use_global_device_ids=true | all-gather | bytes 9216 | tf_op jit(solution)/shard_map/all_gather | solution.py:30
  408.6 5.7 all-gather.38
  414.4 7.0 all-gather.39
  424.8 8.9 %collective-permute-done.20 = f32[3,128,256]{2,1,0:T(8,128)S(1)} collective-permute-done((f32[3,128,256]{2,1,0:T(8,128)S(1)}, f32[3,128,256]{2,1,0:T(8,128)S(1)}, u32[]{:S(2)}, u32[]{:S(2)}) %collective-permute-start.20) | collective-permute-done | bytes 393248 | tf_op jit(solution)/shard_map/ppermute | solution.py:19
  446.9 5.0 collective-permute-done.24
  456.8 5.1 collective-permute-done.26
  469.8 15.6 %collective-permute-done.28 = f32[512,256]{1,0:T(8,128)S(1)} collective-permute-done((f32[512,256]{1,0:T(8,128)S(1)}, f32[512,256]{1,0:T(8,128)S(1)}, u32[]{:S(2)}, u32[]{:S(2)}) %collective-permute-start.28) | collective-permute-done | bytes 524320 | tf_op jit(solution)/shard_map/ppermute | solution.py:19
  494.0 21.2 %collective-permute-done.30 = f32[3,512,256]{2,1,0:T(8,128)S(1)} collective-permute-done((f32[3,512,256]{2,1,0:T(8,128)S(1)}, f32[3,512,256]{2,1,0:T(8,128)S(1)}, u32[]{:S(2)}, u32[]{:S(2)}) %collective-permute-start.30) | collective-permute-done | bytes 1572896 | tf_op jit(solution)/shard_map/ppermute | solution.py:25
  529.7 20.4 %all-gather.40 = f32[8,1,256]{2,1,0:T(1,128)S(1)} all-gather(f32[1,1,256]{2,1,0:T(1,128)S(1)} %bitcast.549), channel_id=12, replica_groups=mesh['gx_0'=8,'gx_1'=2,'gx_2'=2,'gy_0'=2,'gy_1'=4] {'gx_0'}, dimensions={0}, use_global_device_ids=true | all-gather | bytes 9216 | tf_op jit(solution)/shard_map/all_gather | solution.py:30
  556.3 12.0 %all-gather.43 = f32[2,1,256]{2,1,0:T(1,128)S(1)} all-gather(f32[1,1,256]{2,1,0:T(1,128)S(1)} %bitcast.422), channel_id=15, replica_groups=mesh['gx_0'=8,'gx_1'=2,'gx_2'=2,'gy_0'=2,'gy_1'=4] {'gy_0'}, dimensions={0}, use_global_device_ids=true | all-gather | bytes 3072 | tf_op jit(solution)/shard_map/all_gather | solution.py:30
  568.3 9.3 %all-gather.44 = f32[4,1,256]{2,1,0:T(1,128)S(1)} all-gather(f32[1,1,256]{2,1,0:T(1,128)S(1)} %bitcast.423), channel_id=16, replica_groups=mesh['gx_0'=8,'gx_1'=2,'gx_2'=2,'gy_0'=2,'gy_1'=4] {'gy_1'}, dimensions={0}, use_global_device_ids=true | all-gather | bytes 5120 | tf_op jit(solution)/shard_map/all_gather | solution.py:30
  577.6 15.3 %all-gather.45 = f32[8,1,256]{2,1,0:T(1,128)S(1)} all-gather(f32[1,1,256]{2,1,0:T(1,128)S(1)} %bitcast.546), channel_id=17, replica_groups=mesh['gx_0'=8,'gx_1'=2,'gx_2'=2,'gy_0'=2,'gy_1'=4] {'gx_0'}, dimensions={0}, use_global_device_ids=true | all-gather | bytes 9216 | tf_op jit(solution)/shard_map/all_gather | solution.py:30
  599.0 5.7 all-gather.48
  604.8 7.0 all-gather.49
  616.2 8.9 %collective-permute-done.32 = f32[3,128,256]{2,1,0:T(8,128)S(1)} collective-permute-done((f32[3,128,256]{2,1,0:T(8,128)S(1)}, f32[3,128,256]{2,1,0:T(8,128)S(1)}, u32[]{:S(2)}, u32[]{:S(2)}) %collective-permute-start.32) | collective-permute-done | bytes 393248 | tf_op jit(solution)/shard_map/ppermute | solution.py:19
  628.4 5.0 collective-permute-start.35
  639.0 5.3 collective-permute-done.36
  649.4 5.4 collective-permute-done.38
  662.5 16.7 %collective-permute-done.40 = f32[512,256]{1,0:T(8,128)S(1)} collective-permute-done((f32[512,256]{1,0:T(8,128)S(1)}, f32[512,256]{1,0:T(8,128)S(1)}, u32[]{:S(2)}, u32[]{:S(2)}) %collective-permute-start.40) | collective-permute-done | bytes 524320 | tf_op jit(solution)/shard_map/ppermute | solution.py:19
  687.7 21.2 %collective-permute-done.42 = f32[3,512,256]{2,1,0:T(8,128)S(1)} collective-permute-done((f32[3,512,256]{2,1,0:T(8,128)S(1)}, f32[3,512,256]{2,1,0:T(8,128)S(1)}, u32[]{:S(2)}, u32[]{:S(2)}) %collective-permute-start.42) | collective-permute-done | bytes 1572896 | tf_op jit(solution)/shard_map/ppermute | solution.py:25
  722.8 15.2 %all-gather.50 = f32[8,1,256]{2,1,0:T(1,128)S(1)} all-gather(f32[1,1,256]{2,1,0:T(1,128)S(1)} %bitcast.547), channel_id=22, replica_groups=mesh['gx_0'=8,'gx_1'=2,'gx_2'=2,'gy_0'=2,'gy_1'=4] {'gx_0'}, dimensions={0}, use_global_device_ids=true | all-gather | bytes 9216 | tf_op jit(solution)/shard_map/all_gather | solution.py:30
  744.8 17.0 %all-gather.53 = f32[2,1,256]{2,1,0:T(1,128)S(1)} all-gather(f32[1,1,256]{2,1,0:T(1,128)S(1)} %bitcast.430), channel_id=25, replica_groups=mesh['gx_0'=8,'gx_1'=2,'gx_2'=2,'gy_0'=2,'gy_1'=4] {'gy_0'}, dimensions={0}, use_global_device_ids=true | all-gather | bytes 3072 | tf_op jit(solution)/shard_map/all_gather | solution.py:30
  761.8 9.3 %all-gather.54 = f32[4,1,256]{2,1,0:T(1,128)S(1)} all-gather(f32[1,1,256]{2,1,0:T(1,128)S(1)} %bitcast.431), channel_id=26, replica_groups=mesh['gx_0'=8,'gx_1'=2,'gx_2'=2,'gy_0'=2,'gy_1'=4] {'gy_1'}, dimensions={0}, use_global_device_ids=true | all-gather | bytes 5120 | tf_op jit(solution)/shard_map/all_gather | solution.py:30
  771.1 13.3 %all-gather.55 = f32[8,1,256]{2,1,0:T(1,128)S(1)} all-gather(f32[1,1,256]{2,1,0:T(1,128)S(1)} %bitcast.544), channel_id=27, replica_groups=mesh['gx_0'=8,'gx_1'=2,'gx_2'=2,'gy_0'=2,'gy_1'=4] {'gx_0'}, dimensions={0}, use_global_device_ids=true | all-gather | bytes 9216 | tf_op jit(solution)/shard_map/all_gather | solution.py:30
  790.6 5.7 all-gather.58
  796.3 7.0 all-gather.59
  (346 shorter events, 249.2 us)
Async XLA Ops:
  0.7 6.9 collective-permute-start.4
  0.7 6.8 collective-permute-start.5
  3.2 16.9 %collective-permute-start = (f32[3,512]{1,0:T(4,128)S(1)}, f32[3,512]{1,0:T(4,128)S(1)}, u32[]{:S(2)}, u32[]{:S(2)}) collective-permute-start(f32[3,512]{1,0:T(4,128)S(1)} %get-tuple-element.117), channel_id=1, source_target_pairs={{0,8},{8,16},{16,24},{24,32},{32,40},{40,48},{48,56},{56,64},{64,7... | collective-permute-start | bytes 18440 | tf_op jit(solution)/shard_map/ppermute | solution.py:19
  3.4 16.6 %collective-permute-start.1 = (f32[3,512]{1,0:T(4,128)S(1)}, f32[3,512]{1,0:T(4,128)S(1)}, u32[]{:S(2)}, u32[]{:S(2)}) collective-permute-start(f32[3,512]{1,0:T(4,128)S(1)} %get-tuple-element.117), channel_id=1, source_target_pairs={{0,248},{8,0},{16,8},{24,16},{32,24},{40,32},{48,40},{56,48},{64,5... | collective-permute-start | bytes 18440 | tf_op jit(solution)/shard_map/ppermute | solution.py:19
  7.7 6.7 collective-permute-start.7
  9.0 6.3 collective-permute-start.6
  17.0 208.8 %collective-permute-start.8 = (f32[3,128,256]{2,1,0:T(8,128)}, f32[3,128,256]{2,1,0:T(8,128)}, u32[]{:S(2)}, u32[]{:S(2)}) collective-permute-start(f32[3,128,256]{2,1,0:T(8,128)} %pad_maximum_fusion.3), channel_id=1, source_target_pairs={{0,248},{8,0},{16,8},{24,16},{32,24},{40,32},{48,40},{56,48},{64,5... | collective-permute-start | bytes 1179656 | tf_op jit(solution)/shard_map/ppermute | solution.py:19
  20.1 6.6 collective-permute-start.2
  23.5 5.7 collective-permute-start.3
  25.6 200.3 %collective-permute-start.9 = (f32[3,128,256]{2,1,0:T(8,128)}, f32[3,128,256]{2,1,0:T(8,128)}, u32[]{:S(2)}, u32[]{:S(2)}) collective-permute-start(f32[3,128,256]{2,1,0:T(8,128)} %pad_maximum_fusion.4), channel_id=1, source_target_pairs={{0,8},{8,16},{16,24},{24,32},{32,40},{40,48},{48,56},{56,64},{64,7... | collective-permute-start | bytes 1179656 | tf_op jit(solution)/shard_map/ppermute | solution.py:19
  227.1 13.6 %collective-permute-start.10 = (f32[128,256]{1,0:T(8,128)S(1)}, f32[128,256]{1,0:T(8,128)S(1)}, u32[]{:S(2)}, u32[]{:S(2)}) collective-permute-start(f32[128,256]{1,0:T(8,128)S(1)} %get-tuple-element.67), channel_id=1, source_target_pairs={{1,0},{2,1},{3,2},{4,3},{5,4},{6,5},{7,6},{9,8},{10,9},{11,10},{12... | collective-permute-start | bytes 393224 | tf_op jit(solution)/shard_map/ppermute | solution.py:25
  228.4 12.3 %collective-permute-start.11 = (f32[128,256]{1,0:T(8,128)S(1)}, f32[128,256]{1,0:T(8,128)S(1)}, u32[]{:S(2)}, u32[]{:S(2)}) collective-permute-start(f32[128,256]{1,0:T(8,128)S(1)} %get-tuple-element.68), channel_id=1, source_target_pairs={{0,1},{1,2},{2,3},{3,4},{4,5},{5,6},{6,7},{8,9},{9,10},{10,11},{11... | collective-permute-start | bytes 393224 | tf_op jit(solution)/shard_map/ppermute | solution.py:25
  242.5 7.0 collective-permute-start.12
  242.6 6.9 collective-permute-start.13
  249.6 15.0 %collective-permute-start.14 = (f32[3,128,256]{2,1,0:T(8,128)S(1)}, f32[3,128,256]{2,1,0:T(8,128)S(1)}, u32[]{:S(2)}, u32[]{:S(2)}) collective-permute-start(f32[3,128,256]{2,1,0:T(8,128)S(1)} %pad_maximum_fusion.5), channel_id=1, source_target_pairs={{0,1},{1,2},{2,3},{3,4},{4,5},{5,6},{6,7},{8,9},{9,10},{10,11},{11... | collective-permute-start | bytes 1179656 | tf_op jit(solution)/shard_map/ppermute | solution.py:25
  257.3 15.3 %collective-permute-start.15 = (f32[3,128,256]{2,1,0:T(8,128)S(1)}, f32[3,128,256]{2,1,0:T(8,128)S(1)}, u32[]{:S(2)}, u32[]{:S(2)}) collective-permute-start(f32[3,128,256]{2,1,0:T(8,128)S(1)} %pad_maximum_fusion.5), channel_id=1, source_target_pairs={{1,0},{2,1},{3,2},{4,3},{5,4},{6,5},{7,6},{9,8},{10,9},{11,10},{12... | collective-permute-start | bytes 1179656 | tf_op jit(solution)/shard_map/ppermute | solution.py:25
  273.2 61.6 %copy-start.1 = (f32[512,256]{1,0:T(8,128)}, f32[512,256]{1,0:T(8,128)S(1)}, u32[]{:S(2)}) copy-start(f32[512,256]{1,0:T(8,128)S(1)} %convolution_add_fusion.5) | copy-start | bytes 1572868
  273.3 16.7 %collective-permute-start.16 = (f32[512,256]{1,0:T(8,128)S(1)}, f32[512,256]{1,0:T(8,128)S(1)}, u32[]{:S(2)}, u32[]{:S(2)}) collective-permute-start(f32[512,256]{1,0:T(8,128)S(1)} %convolution_add_fusion.5), channel_id=1, source_target_pairs={{0,8},{8,16},{16,24},{24,32},{32,40},{40,48},{48,56},{56,64},{64,7... | collective-permute-start | bytes 1572872 | tf_op jit(solution)/shard_map/ppermute | solution.py:19
  273.4 16.6 %collective-permute-start.17 = (f32[512,256]{1,0:T(8,128)S(1)}, f32[512,256]{1,0:T(8,128)S(1)}, u32[]{:S(2)}, u32[]{:S(2)}) collective-permute-start(f32[512,256]{1,0:T(8,128)S(1)} %convolution_add_fusion.5), channel_id=1, source_target_pairs={{0,248},{8,0},{16,8},{24,16},{32,24},{40,32},{48,40},{56,48},{64,5... | collective-permute-start | bytes 1572872 | tf_op jit(solution)/shard_map/ppermute | solution.py:19
  290.1 34.6 %collective-permute-start.18 = (f32[3,512,256]{2,1,0:T(8,128)S(1)}, f32[3,512,256]{2,1,0:T(8,128)S(1)}, u32[]{:S(2)}, u32[]{:S(2)}) collective-permute-start(f32[3,512,256]{2,1,0:T(8,128)S(1)} %pad_maximum_fusion), channel_id=1, source_target_pairs={{0,1},{1,2},{2,3},{3,4},{4,5},{5,6},{6,7},{8,9},{9,10},{10,11},{11... | collective-permute-start | bytes 4718600 | tf_op jit(solution)/shard_map/ppermute | solution.py:25
  295.4 35.4 %collective-permute-start.19 = (f32[3,512,256]{2,1,0:T(8,128)S(1)}, f32[3,512,256]{2,1,0:T(8,128)S(1)}, u32[]{:S(2)}, u32[]{:S(2)}) collective-permute-start(f32[3,512,256]{2,1,0:T(8,128)S(1)} %pad_maximum_fusion), channel_id=1, source_target_pairs={{1,0},{2,1},{3,2},{4,3},{5,4},{6,5},{7,6},{9,8},{10,9},{11,10},{12... | collective-permute-start | bytes 4718600 | tf_op jit(solution)/shard_map/ppermute | solution.py:25
  424.1 9.6 %collective-permute-start.20 = (f32[3,128,256]{2,1,0:T(8,128)S(1)}, f32[3,128,256]{2,1,0:T(8,128)S(1)}, u32[]{:S(2)}, u32[]{:S(2)}) collective-permute-start(f32[3,128,256]{2,1,0:T(8,128)S(1)} %pad_maximum_fusion.6), channel_id=1, source_target_pairs={{0,248},{8,0},{16,8},{24,16},{32,24},{40,32},{48,40},{56,48},{64,5... | collective-permute-start | bytes 1179656 | tf_op jit(solution)/shard_map/ppermute | solution.py:19
  424.2 10.6 %collective-permute-start.21 = (f32[3,128,256]{2,1,0:T(8,128)S(1)}, f32[3,128,256]{2,1,0:T(8,128)S(1)}, u32[]{:S(2)}, u32[]{:S(2)}) collective-permute-start(f32[3,128,256]{2,1,0:T(8,128)S(1)} %pad_maximum_fusion.7), channel_id=1, source_target_pairs={{0,8},{8,16},{16,24},{24,32},{32,40},{40,48},{48,56},{56,64},{64,7... | collective-permute-start | bytes 1179656 | tf_op jit(solution)/shard_map/ppermute | solution.py:19
  434.9 6.9 collective-permute-start.22
  436.2 7.1 collective-permute-start.23
  445.0 6.8 collective-permute-start.24
  445.1 6.7 collective-permute-start.25
  451.9 10.0 %collective-permute-start.26 = (f32[3,128,256]{2,1,0:T(8,128)S(1)}, f32[3,128,256]{2,1,0:T(8,128)S(1)}, u32[]{:S(2)}, u32[]{:S(2)}) collective-permute-start(f32[3,128,256]{2,1,0:T(8,128)S(1)} %pad_maximum_fusion.8), channel_id=1, source_target_pairs={{0,1},{1,2},{2,3},{3,4},{4,5},{5,6},{6,7},{8,9},{9,10},{10,11},{11... | collective-permute-start | bytes 1179656 | tf_op jit(solution)/shard_map/ppermute | solution.py:25
  454.9 11.1 %collective-permute-start.27 = (f32[3,128,256]{2,1,0:T(8,128)S(1)}, f32[3,128,256]{2,1,0:T(8,128)S(1)}, u32[]{:S(2)}, u32[]{:S(2)}) collective-permute-start(f32[3,128,256]{2,1,0:T(8,128)S(1)} %pad_maximum_fusion.8), channel_id=1, source_target_pairs={{1,0},{2,1},{3,2},{4,3},{5,4},{6,5},{7,6},{9,8},{10,9},{11,10},{12... | collective-permute-start | bytes 1179656 | tf_op jit(solution)/shard_map/ppermute | solution.py:25
  466.7 18.8 %collective-permute-start.28 = (f32[512,256]{1,0:T(8,128)S(1)}, f32[512,256]{1,0:T(8,128)S(1)}, u32[]{:S(2)}, u32[]{:S(2)}) collective-permute-start(f32[512,256]{1,0:T(8,128)S(1)} %convolution_add_fusion.4), channel_id=1, source_target_pairs={{0,8},{8,16},{16,24},{24,32},{32,40},{40,48},{48,56},{56,64},{64,7... | collective-permute-start | bytes 1572872 | tf_op jit(solution)/shard_map/ppermute | solution.py:19
  466.8 18.7 %collective-permute-start.29 = (f32[512,256]{1,0:T(8,128)S(1)}, f32[512,256]{1,0:T(8,128)S(1)}, u32[]{:S(2)}, u32[]{:S(2)}) collective-permute-start(f32[512,256]{1,0:T(8,128)S(1)} %convolution_add_fusion.4), channel_id=1, source_target_pairs={{0,248},{8,0},{16,8},{24,16},{32,24},{40,32},{48,40},{56,48},{64,5... | collective-permute-start | bytes 1572872 | tf_op jit(solution)/shard_map/ppermute | solution.py:19
  485.6 29.7 %collective-permute-start.30 = (f32[3,512,256]{2,1,0:T(8,128)S(1)}, f32[3,512,256]{2,1,0:T(8,128)S(1)}, u32[]{:S(2)}, u32[]{:S(2)}) collective-permute-start(f32[3,512,256]{2,1,0:T(8,128)S(1)} %pad_maximum_fusion.1), channel_id=1, source_target_pairs={{0,1},{1,2},{2,3},{3,4},{4,5},{5,6},{6,7},{8,9},{9,10},{10,11},{11... | collective-permute-start | bytes 4718600 | tf_op jit(solution)/shard_map/ppermute | solution.py:25
  487.0 35.9 %collective-permute-start.31 = (f32[3,512,256]{2,1,0:T(8,128)S(1)}, f32[3,512,256]{2,1,0:T(8,128)S(1)}, u32[]{:S(2)}, u32[]{:S(2)}) collective-permute-start(f32[3,512,256]{2,1,0:T(8,128)S(1)} %pad_maximum_fusion.1), channel_id=1, source_target_pairs={{1,0},{2,1},{3,2},{4,3},{5,4},{6,5},{7,6},{9,8},{10,9},{11,10},{12... | collective-permute-start | bytes 4718600 | tf_op jit(solution)/shard_map/ppermute | solution.py:25
  615.5 9.6 %collective-permute-start.32 = (f32[3,128,256]{2,1,0:T(8,128)S(1)}, f32[3,128,256]{2,1,0:T(8,128)S(1)}, u32[]{:S(2)}, u32[]{:S(2)}) collective-permute-start(f32[3,128,256]{2,1,0:T(8,128)S(1)} %pad_maximum_fusion.9), channel_id=1, source_target_pairs={{0,248},{8,0},{16,8},{24,16},{32,24},{40,32},{48,40},{56,48},{64,5... | collective-permute-start | bytes 1179656 | tf_op jit(solution)/shard_map/ppermute | solution.py:19
  615.7 11.3 %collective-permute-start.33 = (f32[3,128,256]{2,1,0:T(8,128)S(1)}, f32[3,128,256]{2,1,0:T(8,128)S(1)}, u32[]{:S(2)}, u32[]{:S(2)}) collective-permute-start(f32[3,128,256]{2,1,0:T(8,128)S(1)} %pad_maximum_fusion.10), channel_id=1, source_target_pairs={{0,8},{8,16},{16,24},{24,32},{32,40},{40,48},{48,56},{56,64},{64,7... | collective-permute-start | bytes 1179656 | tf_op jit(solution)/shard_map/ppermute | solution.py:19
  627.1 6.9 collective-permute-start.34
  628.4 7.1 collective-permute-start.35
  637.2 7.1 collective-permute-start.36
  637.3 7.0 collective-permute-start.37
  644.4 10.5 %collective-permute-start.38 = (f32[3,128,256]{2,1,0:T(8,128)S(1)}, f32[3,128,256]{2,1,0:T(8,128)S(1)}, u32[]{:S(2)}, u32[]{:S(2)}) collective-permute-start(f32[3,128,256]{2,1,0:T(8,128)S(1)} %pad_maximum_fusion.11), channel_id=1, source_target_pairs={{0,1},{1,2},{2,3},{3,4},{4,5},{5,6},{6,7},{8,9},{9,10},{10,11},{11... | collective-permute-start | bytes 1179656 | tf_op jit(solution)/shard_map/ppermute | solution.py:25
  647.5 12.0 %collective-permute-start.39 = (f32[3,128,256]{2,1,0:T(8,128)S(1)}, f32[3,128,256]{2,1,0:T(8,128)S(1)}, u32[]{:S(2)}, u32[]{:S(2)}) collective-permute-start(f32[3,128,256]{2,1,0:T(8,128)S(1)} %pad_maximum_fusion.11), channel_id=1, source_target_pairs={{1,0},{2,1},{3,2},{4,3},{5,4},{6,5},{7,6},{9,8},{10,9},{11,10},{12... | collective-permute-start | bytes 1179656 | tf_op jit(solution)/shard_map/ppermute | solution.py:25
  660.2 19.0 %collective-permute-start.40 = (f32[512,256]{1,0:T(8,128)S(1)}, f32[512,256]{1,0:T(8,128)S(1)}, u32[]{:S(2)}, u32[]{:S(2)}) collective-permute-start(f32[512,256]{1,0:T(8,128)S(1)} %convolution_add_fusion.3), channel_id=1, source_target_pairs={{0,8},{8,16},{16,24},{24,32},{32,40},{40,48},{48,56},{56,64},{64,7... | collective-permute-start | bytes 1572872 | tf_op jit(solution)/shard_map/ppermute | solution.py:19
  660.2 18.9 %collective-permute-start.41 = (f32[512,256]{1,0:T(8,128)S(1)}, f32[512,256]{1,0:T(8,128)S(1)}, u32[]{:S(2)}, u32[]{:S(2)}) collective-permute-start(f32[512,256]{1,0:T(8,128)S(1)} %convolution_add_fusion.3), channel_id=1, source_target_pairs={{0,248},{8,0},{16,8},{24,16},{32,24},{40,32},{48,40},{56,48},{64,5... | collective-permute-start | bytes 1572872 | tf_op jit(solution)/shard_map/ppermute | solution.py:19
  679.3 29.7 %collective-permute-start.42 = (f32[3,512,256]{2,1,0:T(8,128)S(1)}, f32[3,512,256]{2,1,0:T(8,128)S(1)}, u32[]{:S(2)}, u32[]{:S(2)}) collective-permute-start(f32[3,512,256]{2,1,0:T(8,128)S(1)} %pad_maximum_fusion.2), channel_id=1, source_target_pairs={{0,1},{1,2},{2,3},{3,4},{4,5},{5,6},{6,7},{8,9},{9,10},{10,11},{11... | collective-permute-start | bytes 4718600 | tf_op jit(solution)/shard_map/ppermute | solution.py:25
  680.7 35.3 %collective-permute-start.43 = (f32[3,512,256]{2,1,0:T(8,128)S(1)}, f32[3,512,256]{2,1,0:T(8,128)S(1)}, u32[]{:S(2)}, u32[]{:S(2)}) collective-permute-start(f32[3,512,256]{2,1,0:T(8,128)S(1)} %pad_maximum_fusion.2), channel_id=1, source_target_pairs={{1,0},{2,1},{3,2},{4,3},{5,4},{6,5},{7,6},{9,8},{10,9},{11,10},{12... | collective-permute-start | bytes 4718600 | tf_op jit(solution)/shard_map/ppermute | solution.py:25
  719.8 83.5 %copy-start.2 = (f32[512,256]{1,0:T(8,128)S(1)}, f32[512,256]{1,0:T(8,128)}, u32[]{:S(2)}) copy-start(f32[512,256]{1,0:T(8,128)} %copy-done.1) | copy-start | bytes 1572868
  719.9 83.5 %copy-start.4 = (f32[512,256]{1,0:T(8,128)S(1)}, f32[512,256]{1,0:T(8,128)}, u32[]{:S(2)}) copy-start(f32[512,256]{1,0:T(8,128)} %copy-done.3) | copy-start | bytes 1572868
  719.9 83.5 %copy-start.6 = (f32[512,256]{1,0:T(8,128)S(1)}, f32[512,256]{1,0:T(8,128)}, u32[]{:S(2)}) copy-start(f32[512,256]{1,0:T(8,128)} %get-tuple-element.135) | copy-start | bytes 1572868
  (25 other events, 365.4 us)
